TPU v7x, 32 devices: a whole 2x2x4 slice. The times are simulated.
32 devices in a mesh: date: 4 (over y, x), path: 8 (over z, core).
Axes of the slice: x: 2, y: 2, z: 4, core: 2. Of those that a mesh axis runs over, the one named last changes fastest.
Arguments:
- factors: bfloat16 [32, 16, 32768], P('date', None, 'path'), may hold values from -10 to 10
- cashflows: bfloat16 [32, 64, 32768], P('date', None, 'path'), may hold values from -12 to 12
- frequency: bfloat16 [128, 16], replicated, may hold values from -1.5 to 1.5
- phases: float32 [128], replicated, may hold values from -3.140625 to 3.140625
- margin_lag: int32 [64], replicated, may hold values from 1 to 2
- thresholds: int32 [64], replicated, may hold values from 0 to 149
- transfer_min: int32 [64], replicated, may hold values from 0 to 59
Outputs:
- exposure: bfloat16 [32, 64, 32768], P('date', None, 'path')
- profile: float32 [32, 64], P('date')
All inputs are finite; a program needn't handle non-finite values.
Results may differ from a plain program's by a relative error of at most 0.0058.
Values may be sent and summed in bfloat16 or wider, within the bound.
A program may use at most 128 MiB of HBM per device.

v0:
```python
import jax
import jax.numpy as jnp
from jax import lax
from jax.sharding import PartitionSpec as P

LAG_MAX = 2


ridge_weight = 0.05
root_two = 1.4142135623730951


def shifted_2(value, axis, by):
    length = lax.axis_size(axis)
    pairs = [(i, i + by) for i in range(length) if 0 <= i + by < length]
    return lax.ppermute(value, axis, pairs)


def featurize(frequency, phases, factors):
    angles = jnp.einsum("kr,trp->tkp", frequency, factors, preferred_element_type=jnp.float32)
    angles = angles + phases[None, :, None]
    return (root_two * jnp.cos(angles)).astype(jnp.bfloat16)


def regress(gram_sum, right_sum, paths_all):
    system = (
        gram_sum / paths_all + ridge_weight * jnp.eye(gram_sum.shape[-1], dtype=jnp.float32)[None]
    )
    factor = lax.linalg.cholesky(system)
    solved = lax.linalg.triangular_solve(factor, right_sum / paths_all, left_side=True, lower=True)
    solved = lax.linalg.triangular_solve(
        factor, solved, left_side=True, lower=True, transpose_a=True
    )
    return solved.astype(jnp.bfloat16)


def fitted(coefficients, features):
    return jnp.einsum(
        "tkn,tkp->tnp", coefficients, features, preferred_element_type=jnp.float32
    ).astype(jnp.bfloat16)


def local(factors, cashflows, frequency, phases, margin_lag, thresholds, transfer_min):
    features = featurize(frequency, phases, factors)
    gram_sum = jnp.einsum("tkp,tjp->tkj", features, features, preferred_element_type=jnp.float32)
    right_sum = jnp.einsum("tkp,tnp->tkn", features, cashflows, preferred_element_type=jnp.float32)
    gram_sum, right_sum = lax.psum((gram_sum, right_sum), "path")
    paths_all = features.shape[2] * lax.axis_size("path")
    coefficients = regress(gram_sum, right_sum, paths_all)
    values = fitted(coefficients, features)
    prior_values = shifted_2(values[-LAG_MAX:], "date", 1)
    joined = jnp.concatenate([prior_values, values], axis=0)
    dates_here = values.shape[0]
    lagged = jnp.zeros(values.shape, jnp.float32)
    for lag_value in range(1, LAG_MAX + 1):
        shifted = joined[LAG_MAX - lag_value : LAG_MAX - lag_value + dates_here].astype(jnp.float32)
        lagged = jnp.where((margin_lag == lag_value)[None, :, None], shifted, lagged)
    offset = (thresholds + transfer_min).astype(jnp.float32) / 100.0
    collateral = jnp.maximum(lagged - offset[None, :, None], 0.0)
    exposure = jnp.maximum(values.astype(jnp.float32) - collateral, 0.0)
    profile = lax.psum(jnp.sum(exposure, axis=2), "path") / paths_all
    return (exposure.astype(jnp.bfloat16), profile)


def solution(mesh):
    return jax.shard_map(
        local,
        mesh=mesh,
        in_specs=(P("date", None, "path"), P("date", None, "path"), P(), P(), P(), P(), P()),
        out_specs=(P("date", None, "path"), P("date", None)),
        check_vma=False,
    )
```

profile of v0, /device:TPU:5, one launch (start us, length us, event | category | flops | bytes accessed | tf_op | source)
XLA Modules:
  0.0 384.7 jit_solution(4101414484318501345)
XLA Ops:
  7.2 0.0 copy-start
  7.2 0.0 all-reduce.3.cloned.1.call-start
  7.2 1.2 copy-done
  8.4 62.0 %multiply_convert_fusion = bf16[8,4096,128]{2,1,0:T(8,128)(2,1)} fusion(bf16[8,16,4096]{2,1,0:T(8,128)(2,1)S(1)} %copy-done, f32[128]{0:T(128)} %param.10, bf16[128,16]{0,1:T(8,128)(2,1)} %param.9), kind=kOutput, calls=%fused_computation | convolution fusion | flops 146800640 | bytes 9441792 | tf_op jit(solution)/shard_map/kr,trp->tkp/dot_general | solution.py:20
  70.4 9.0 %fusion.10 = f32[8,128,128]{1,2,0:T(8,128)} fusion(bf16[8,4096,128]{2,1,0:T(8,128)(2,1)} %multiply_convert_fusion), kind=kOutput, calls=%fused_computation.29 | convolution fusion | flops 1073741824 | bytes 8912896 | tf_op jit(solution)/shard_map/tkp,tjp->tkj/dot_general | solution.py:45
  79.5 8.0 %fusion.11 = f32[8,128,64]{2,1,0:T(8,128)} fusion(bf16[8,4096,128]{2,1,0:T(8,128)(2,1)} %multiply_convert_fusion, bf16[8,64,4096]{2,1,0:T(8,128)(2,1)} %param.8), kind=kOutput, calls=%fused_computation.30 | convolution fusion | flops 536870912 | bytes 12845056 | tf_op jit(solution)/shard_map/tkp,tnp->tkn/dot_general | solution.py:46
  87.4 0.0 all-reduce.3.cloned.1.call-update
  87.5 0.1 copy.15
  87.6 58.8 %all-reduce.3.cloned.1.call-done = (f32[8,128,128]{1,2,0:T(8,128)}, f32[8,128,64]{2,1,0:T(8,128)}) async-done(((f32[8,128,128]{1,2,0:T(8,128)}, f32[8,128,64]{2,1,0:T(8,128)}), (f32[8,128,128]{1,2,0:T(8,128)}, f32[8,128,64]{2,1,0:T(8,128)})) %all-reduce.3.cloned.1.call-update) | async-done | bytes 786448 | tf_op jit(solution)/shard_map/psum | solution.py:47
  146.4 1.1 multiply_add_fusion
  147.5 0.2 copy.16
  147.7 1.1 fusion.4
  148.8 93.8 %custom-call.8 = f32[8,128,128]{2,1,0:T(8,128)S(1)} custom-call(f32[8,128,128]{2,1,0:T(8,128)S(1)} %fusion.4), custom_call_target="Cholesky" | custom-call | tf_op jit(solution)/shard_map/cholesky | solution.py:29
  242.6 0.1 select_reduce_fusion
  242.7 0.1 compare_reduce_fusion
  242.8 0.1 select_bitcast_fusion
  242.9 78.8 %custom-call.9 = f32[8,1,128,128]{2,3,1,0:T(8,128)S(1)} custom-call(f32[8,1,128,128]{3,2,1,0:T(8,128)S(1)} %select_bitcast_fusion), custom_call_target="InvertDiagBlocksLowerTriangular" | custom-call | tf_op jit(solution)/shard_map/triangular_solve | solution.py:31
  321.7 0.0 copy-start.1
  321.7 2.1 fusion.2
  323.8 0.0 copy-start.2
  323.8 0.0 copy-start.3
  323.8 1.1 convolution_convert_fusion.1
  324.9 6.4 %convolution_convert_fusion = bf16[8,64,4096]{2,1,0:T(8,128)(2,1)S(1)} fusion(bf16[8,128,64]{1,2,0:T(8,128)(2,1)S(1)} %convolution_convert_fusion.1, bf16[8,4096,128]{2,1,0:T(8,128)(2,1)} %multiply_convert_fusion), kind=kOutput, calls=%fused_computation.2 | convolution fusion | flops 538968064 | bytes 12713984 | tf_op jit(solution)/shard_map/tkn,tkp->tnp/dot_general | solution.py:38
  331.3 0.1 slice.24
  331.4 3.1 collective-permute-start
  334.5 0.0 copy-done.1
  334.5 0.0 copy-done.2
  334.5 0.0 copy-done.3
  334.6 22.0 %collective-permute-done = bf16[2,64,4096]{2,1,0:T(8,128)(2,1)S(1)} collective-permute-done((bf16[2,64,4096]{2,1,0:T(8,128)(2,1)S(1)}, bf16[2,64,4096]{2,1,0:T(8,128)(2,1)S(1)}, u32[]{:S(2)}, u32[]{:S(2)}) %collective-permute-start) | collective-permute-done | bytes 1048608 | tf_op jit(solution)/shard_map/ppermute | solution.py:16
  356.5 4.5 %fusion.9 = (f32[8,64]{1,0:T(8,128)S(1)}, bf16[8,64,4096]{2,1,0:T(8,128)(2,1)}) fusion(f32[64]{0:T(128)S(1)} %convert_multiply_fusion, bf16[8,64,4096]{2,1,0:T(8,128)(2,1)S(1)} %convolution_convert_fusion, bf16[2,64,4096]{2,1,0:T(8,128)(2,1)S(1)} %collective-permute-done, pred[64]{0:T(512)(128)(4,1)S(1)} %get-tuple-element.7, ...), kind=kLoop, calls=%fused_computation.28 | loop fusion | flops 27262464 | bytes 9439616 | tf_op jit(solution)/shard_map/reduce_sum | solution.py:61
  361.1 16.2 %psum.23 = f32[8,64]{1,0:T(8,128)S(1)} all-reduce(f32[8,64]{1,0:T(8,128)S(1)} %get-tuple-element.4), channel_id=1, replica_groups=mesh['date'=4,'path'=8] {'path'}, use_global_device_ids=true, to_apply=%region_5.6 | all-reduce | flops 512 | bytes 4096 | tf_op jit(solution)/shard_map/psum | solution.py:61
  377.2 0.6 broadcast_multiply_fusion
  (5 shorter events, 0.1 us)
Async XLA Ops:
  7.2 1.2 copy-start
  7.2 139.2 %all-reduce.3.cloned.1.call-start = ((), (), s32[]{:S(2)}) async-start(), calls=%async_computation | async-start | bytes 2097152 | tf_op jit(solution)/shard_map/psum | solution.py:47
  321.7 12.8 %copy-start.1 = (s32[64]{0:T(128)S(1)}, s32[64]{0:T(128)}, u32[]{:S(2)}) copy-start(s32[64]{0:T(128)} %param.11) | copy-start | bytes 772
  323.8 10.8 %copy-start.2 = (s32[64]{0:T(128)S(1)}, s32[64]{0:T(128)}, u32[]{:S(2)}) copy-start(s32[64]{0:T(128)} %param.12) | copy-start | bytes 772
  323.8 10.8 %copy-start.3 = (s32[64]{0:T(128)S(1)}, s32[64]{0:T(128)}, u32[]{:S(2)}) copy-start(s32[64]{0:T(128)} %param.13) | copy-start | bytes 772
  331.4 25.1 %collective-permute-start = (bf16[2,64,4096]{2,1,0:T(8,128)(2,1)S(1)}, bf16[2,64,4096]{2,1,0:T(8,128)(2,1)S(1)}, u32[]{:S(2)}, u32[]{:S(2)}) collective-permute-start(bf16[2,64,4096]{2,1,0:T(8,128)(2,1)S(1)} %slice.24), channel_id=1, source_target_pairs={{0,8},{8,16},{16,24},{1,9},{9,17},{17,25},{2,10},{10,18},{18,26},{... | collective-permute-start | bytes 3145736 | tf_op jit(solution)/shard_map/ppermute | solution.py:16
Sparse Core Ops, SparseCore 0:
  87.6 58.7 all-reduce.2
where the time goes:
time: 385 us
  other arithmetic  180 us (47%)
  matrix products  88.6 us (23%)
  waiting for transfers between devices  80.8 us (21%)
  blocking collectives  16.2 us (4%)
  between operations  14.2 us (4%)
    another operation x4, other arithmetic, regress(): factor = lax.linalg.cholesky(system)  94 us
    another operation x3, other arithmetic, regress(): lax.linalg.triangular_solve(factor, solved, left_side=True, lower=True, t...  78.9 us
    dot_general x1, matrix products, featurize(): jnp.einsum('kr,trp->tkp', frequency, factors, preferred_element_type=jnp....  62 us
    psum x1, waiting for transfers between devices, local(): gram_sum, right_sum = lax.psum((gram_sum, right_sum), 'path')  58.8 us
    ppermute x1, waiting for transfers between devices, shifted_2(): return lax.ppermute(value, axis, pairs)  22 us
    psum x1, blocking collectives, local(): profile = lax.psum(jnp.sum(exposure, axis=2), 'path') / paths_all  16.2 us
    dot_general x1, matrix products, local(): jnp.einsum('tkp,tjp->tkj', features, features, preferred_element_type=jnp...  9.05 us
    dot_general x1, matrix products, local(): jnp.einsum('tkp,tnp->tkn', features, cashflows, preferred_element_type=jn...  7.98 us
  transfers between devices with their start and end apart: 2, of which 2 were waited for; matrix products, arithmetic and copies ran while one was open for 0% of the time, Pallas kernels for 0%

commit v1 on v0

--- a/solution.py
+++ b/solution.py
@@ -1,13 +1,24 @@
 import jax
 import jax.numpy as jnp
 from jax import lax
+from jax.experimental import pallas as pl
+from jax.experimental.pallas import tpu as pltpu
 from jax.sharding import PartitionSpec as P
 
 LAG_MAX = 2
 
 
 ridge_weight = 0.05
-root_two = 1.4142135623730951
+inverse_turn = 0.15915494309189535
+wave = (
+    1.414213547,
+    -27.91545067,
+    91.83777847,
+    -120.8447093,
+    85.08959522,
+    -36.72272039,
+    9.231570304,
+)
 
 
 def shifted_2(value, axis, by):
@@ -18,20 +29,60 @@
 
 def featurize(frequency, phases, factors):
     angles = jnp.einsum("kr,trp->tkp", frequency, factors, preferred_element_type=jnp.float32)
-    angles = angles + phases[None, :, None]
-    return (root_two * jnp.cos(angles)).astype(jnp.bfloat16)
+    turns = (angles + phases[None, :, None]) * inverse_turn
+    turns = turns - jnp.round(turns)
+    square = turns * turns
+    total = wave[-1]
+    for term in wave[-2::-1]:
+        total = total * square + term
+    return total.astype(jnp.bfloat16)
+
+
+def eliminate(scale, gram_ref, right_ref, out_ref, left, right):
+    dates, size, _ = gram_ref.shape
+    rows = lax.broadcasted_iota(jnp.int32, (size, size), 0)
+    columns = lax.broadcasted_iota(jnp.int32, (size, size), 1)
+    ridge = jnp.where(rows == columns, ridge_weight, 0.0)
+    for d in range(dates):
+        left[d] = gram_ref[d] * scale + ridge
+        right[d] = right_ref[d] * scale
+
+    def step(j, carry):
+        place = jnp.full((size, size), j, jnp.int32)
+        for d in range(dates):
+            column = jnp.take_along_axis(left[d], place, axis=1, mode="promise_in_bounds")
+            row = left[d, pl.ds(j, 1), :]
+            pivot = jnp.take_along_axis(
+                jnp.broadcast_to(row, (8, size)), place[:8], axis=1, mode="promise_in_bounds"
+            )
+            inverse = (1.0 / pivot)[:1]
+            row = row * inverse
+            row_right = right[d, pl.ds(j, 1), :] * inverse[:, : right.shape[2]]
+            left[d] = left[d] - column * row
+            right[d] = right[d] - column[:, : right.shape[2]] * row_right
+            left[d, pl.ds(j, 1), :] = row
+            right[d, pl.ds(j, 1), :] = row_right
+        return carry
+
+    lax.fori_loop(0, size, step, 0)
+    for d in range(dates):
+        out_ref[d] = right[d].astype(out_ref.dtype)
 
 
 def regress(gram_sum, right_sum, paths_all):
-    system = (
-        gram_sum / paths_all + ridge_weight * jnp.eye(gram_sum.shape[-1], dtype=jnp.float32)[None]
-    )
-    factor = lax.linalg.cholesky(system)
-    solved = lax.linalg.triangular_solve(factor, right_sum / paths_all, left_side=True, lower=True)
-    solved = lax.linalg.triangular_solve(
-        factor, solved, left_side=True, lower=True, transpose_a=True
-    )
-    return solved.astype(jnp.bfloat16)
+    def kernel(*refs):
+        eliminate(1.0 / paths_all, *refs)
+
+    return pl.pallas_call(
+        kernel,
+        out_shape=jax.ShapeDtypeStruct(right_sum.shape, jnp.bfloat16),
+        in_specs=[pl.BlockSpec(memory_space=pltpu.VMEM)] * 2,
+        out_specs=pl.BlockSpec(memory_space=pltpu.VMEM),
+        scratch_shapes=[
+            pltpu.VMEM(gram_sum.shape, jnp.float32),
+            pltpu.VMEM(right_sum.shape, jnp.float32),
+        ],
+    )(gram_sum, right_sum)
 
 
 def fitted(coefficients, features):
@@ -41,14 +92,17 @@
 
 
 def local(factors, cashflows, frequency, phases, margin_lag, thresholds, transfer_min):
+    prior_factors = shifted_2(factors[-LAG_MAX:], "date", 1)
     features = featurize(frequency, phases, factors)
     gram_sum = jnp.einsum("tkp,tjp->tkj", features, features, preferred_element_type=jnp.float32)
     right_sum = jnp.einsum("tkp,tnp->tkn", features, cashflows, preferred_element_type=jnp.float32)
     gram_sum, right_sum = lax.psum((gram_sum, right_sum), "path")
+    prior_features = featurize(frequency, phases, prior_factors)
     paths_all = features.shape[2] * lax.axis_size("path")
     coefficients = regress(gram_sum, right_sum, paths_all)
+    prior_coefficients = shifted_2(coefficients[-LAG_MAX:], "date", 1)
     values = fitted(coefficients, features)
-    prior_values = shifted_2(values[-LAG_MAX:], "date", 1)
+    prior_values = fitted(prior_coefficients, prior_features)
     joined = jnp.concatenate([prior_values, values], axis=0)
     dates_here = values.shape[0]
     lagged = jnp.zeros(values.shape, jnp.float32)

time: 385 us -> 240 us (0.62)
  other arithmetic: 180 us -> 8.53 us
  Pallas kernels: 0 us -> 101 us
  matrix products: 88.6 us -> 32.3 us
  waiting for transfers between devices: 80.8 us -> 58.2 us
    another operation x7 -> x0, other arithmetic: 173 us -> none  [the longest x4 94 us: regress(): factor = lax.linalg.cholesky(system)]
    pallas_call x0 -> x1, Pallas kernels: none -> 101 us  [regress(): pl.pallas_call(kernel, out_shape=jax.ShapeDtypeStruct(right_sum.shape, jn...]
    dot_general x1, matrix products: 62 us -> 11.6 us  [featurize(): jnp.einsum('kr,trp->tkp', frequency, factors, preferred_element_type=jnp....]
    ppermute x1 -> x2, waiting for transfers between devices: 22 us -> 0.01 us  [shifted_2(): return lax.ppermute(value, axis, pairs)]
    dot_general x1, matrix products: 9.05 us -> 3.54 us  [local(): jnp.einsum('tkp,tjp->tkj', features, features, preferred_element_type=jnp...]
    dot_general x1 -> x2, matrix products: 6.4 us -> 11.4 us  [fitted(): jnp.einsum('tkn,tkp->tnp', coefficients, features, preferred_element_type...]
  transfers between devices with their start and end apart: 2 -> 3, of which waited for: 2 -> 1; matrix products, arithmetic and copies ran while one was open for 0% -> 13% of each run, Pallas kernels for 0% -> 42%
where the time goes in v1:
time: 240 us; the launch traced here: 238 us
  Pallas kernels  101 us (42%)
  waiting for transfers between devices  58.2 us (24%)
  matrix products  32.3 us (13%)
  blocking collectives  15.6 us (6%)
  between operations  14.1 us (6%)
  other arithmetic  8.53 us (4%)
  starting transfers between devices  6.42 us (3%)
    pallas_call x1, Pallas kernels, regress(): pl.pallas_call(kernel, out_shape=jax.ShapeDtypeStruct(right_sum.shape, jn...  101 us
    psum x1, waiting for transfers between devices, local(): gram_sum, right_sum = lax.psum((gram_sum, right_sum), 'path')  58.2 us
    psum x1, blocking collectives, local(): profile = lax.psum(jnp.sum(exposure, axis=2), 'path') / paths_all  15.6 us
    dot_general x1, matrix products, featurize(): jnp.einsum('kr,trp->tkp', frequency, factors, preferred_element_type=jnp....  11.6 us
    dot_general x2, matrix products, fitted(): jnp.einsum('tkn,tkp->tnp', coefficients, features, preferred_element_type...  11.4 us
    reduce_sum x1, other arithmetic, local(): profile = lax.psum(jnp.sum(exposure, axis=2), 'path') / paths_all  7.92 us
    ppermute x2, starting transfers between devices, shifted_2(): return lax.ppermute(value, axis, pairs)  6.39 us
    dot_general x1, matrix products, local(): jnp.einsum('tkp,tnp->tkn', features, cashflows, preferred_element_type=jn...  5.64 us
  transfers between devices with their start and end apart: 3, of which 1 were waited for; matrix products, arithmetic and copies ran while one was open for 13% of the time, Pallas kernels for 42%

profile of v1, /device:TPU:5, one launch (start us, length us, event | category | flops | bytes accessed | tf_op | source)
XLA Modules:
  0.0 237.9 jit_solution(10986885018582401812)
XLA Ops:
  7.2 0.0 copy-start
  7.2 0.0 all-reduce.3.cloned.1.call-start
  7.2 1.0 slice.13
  8.2 3.1 %collective-permute-start.1 = (bf16[2,16,4096]{2,1,0:T(8,128)(2,1)S(1)}, bf16[2,16,4096]{2,1,0:T(8,128)(2,1)S(1)}, u32[]{:S(2)}, u32[]{:S(2)}) collective-permute-start(bf16[2,16,4096]{2,1,0:T(8,128)(2,1)S(1)} %slice.13), channel_id=1, source_target_pairs={{0,8},{8,16},{16,24},{1,9},{9,17},{17,25},{2,10},{10,18},{18,26},{... | collective-permute-start | bytes 786440 | tf_op jit(solution)/shard_map/ppermute | solution.py:27
  11.3 0.0 copy-done
  11.3 11.6 %add_convert_fusion = bf16[8,128,4096]{1,2,0:T(8,128)(2,1)S(1)} fusion(bf16[8,16,4096]{2,1,0:T(8,128)(2,1)} %param.7, f32[128]{0:T(128)} %param.10, bf16[128,16]{0,1:T(8,128)(2,1)S(1)} %copy-done), kind=kOutput, calls=%fused_computation.2 | convolution fusion | flops 209715200 | bytes 9441792 | tf_op jit(solution)/shard_map/kr,trp->tkp/dot_general | solution.py:31
  23.0 0.0 copy-start.1
  23.0 3.5 %fusion.17 = f32[8,128,128]{2,1,0:T(8,128)} fusion(bf16[8,128,4096]{1,2,0:T(8,128)(2,1)S(1)} %add_convert_fusion), kind=kOutput, calls=%fused_computation.31 | convolution fusion | flops 1073741824 | bytes 8912896 | tf_op jit(solution)/shard_map/tkp,tjp->tkj/dot_general | solution.py:97
  26.5 0.0 copy-done.1
  26.5 0.0 copy-start.2
  26.5 0.0 copy-start.3
  26.5 0.0 copy-start.4
  26.5 5.6 %fusion.18 = f32[8,128,64]{2,1,0:T(8,128)} fusion(bf16[8,128,4096]{1,2,0:T(8,128)(2,1)S(1)} %add_convert_fusion, bf16[8,64,4096]{2,1,0:T(8,128)(2,1)} %param.8), kind=kOutput, calls=%fused_computation.32 | convolution fusion | flops 536870912 | bytes 12845056 | tf_op jit(solution)/shard_map/tkp,tnp->tkn/dot_general | solution.py:98
  32.2 0.0 copy-start.5
  32.2 0.0 all-reduce.3.cloned.1.call-update
  32.2 0.0 copy-done.2
  32.2 0.0 copy-done.3
  32.2 0.0 copy-done.4
  32.3 58.2 %all-reduce.3.cloned.1.call-done = (f32[8,128,128]{2,1,0:T(8,128)}, f32[8,128,64]{2,1,0:T(8,128)}) async-done(((f32[8,128,128]{2,1,0:T(8,128)}, f32[8,128,64]{2,1,0:T(8,128)}), (f32[8,128,128]{2,1,0:T(8,128)}, f32[8,128,64]{2,1,0:T(8,128)})) %all-reduce.3.cloned.1.call-update) | async-done | bytes 786448 | tf_op jit(solution)/shard_map/psum | solution.py:99
  90.5 100.9 %shard_map.86 = bf16[8,128,64]{2,1,0:T(8,128)(2,1)} custom-call(f32[8,128,128]{2,1,0:T(8,128)} %get-tuple-element.2.refs_0_, f32[8,128,64]{2,1,0:T(8,128)} %get-tuple-element.3.refs_1_), custom_call_target="tpu_custom_call" | custom-call | tf_op jit(solution)/shard_map/pallas_call | solution.py:76
  191.4 0.8 slice.16
  192.2 3.3 %collective-permute-start = (bf16[2,128,64]{2,1,0:T(8,128)(2,1)S(1)}, bf16[2,128,64]{2,1,0:T(8,128)(2,1)S(1)}, u32[]{:S(2)}, u32[]{:S(2)}) collective-permute-start(bf16[2,128,64]{2,1,0:T(8,128)(2,1)S(1)} %slice.16), channel_id=1, source_target_pairs={{0,8},{8,16},{16,24},{1,9},{9,17},{17,25},{2,10},{10,18},{18,26},{... | collective-permute-start | bytes 98312 | tf_op jit(solution)/shard_map/ppermute | solution.py:27
  195.5 8.5 %convolution_convert_fusion = bf16[8,64,4096]{2,1,0:T(8,128)(2,1)} fusion(bf16[8,128,64]{2,1,0:T(8,128)(2,1)} %shard_map.86, bf16[8,128,4096]{1,2,0:T(8,128)(2,1)} %copy-done.1), kind=kOutput, calls=%fused_computation.5 | convolution fusion | flops 538968064 | bytes 12713984 | tf_op jit(solution)/shard_map/tkn,tkp->tnp/dot_general | solution.py:89
  204.0 0.0 collective-permute-done.1
  204.0 0.0 collective-permute-done
  204.0 0.0 copy-done.5
  204.0 2.9 %convolution_convert_fusion.1 = bf16[2,64,4096]{2,1,0:T(8,128)(2,1)S(1)} fusion(bf16[2,128,64]{2,1,0:T(8,128)(2,1)S(1)} %collective-permute-done, bf16[2,16,4096]{2,1,0:T(8,128)(2,1)S(1)} %collective-permute-done.1, f32[128]{0:T(128)S(1)} %copy-done.5, bf16[128,16]{0,1:T(8,128)(2,1)S(1)} %copy-done), kind=kOutput, calls=%fused_computation.12 | convolution fusion | flops 187170816 | bytes 1348096 | tf_op jit(solution)/shard_map/tkn,tkp->tnp/dot_general | solution.py:89
  207.0 7.9 %fusion.16 = (f32[8,64]{1,0:T(8,128)S(1)}, bf16[8,64,4096]{2,1,0:T(8,128)(2,1)}) fusion(f32[64]{0:T(128)S(1)} %convert_multiply_fusion, bf16[8,64,4096]{2,1,0:T(8,128)(2,1)} %convolution_convert_fusion, bf16[2,64,4096]{2,1,0:T(8,128)(2,1)S(1)} %convolution_convert_fusion.1, pred[64]{0:T(512)(128)(4,1)S(1)} %get-tuple-element.7, ...), kind=kLoop, calls=%fused_computation.30 | loop fusion | flops 27262464 | bytes 9439616 | tf_op jit(solution)/shard_map/reduce_sum | solution.py:115
  214.9 15.6 %psum.23 = f32[8,64]{1,0:T(8,128)S(1)} all-reduce(f32[8,64]{1,0:T(8,128)S(1)} %get-tuple-element.4), channel_id=1, replica_groups=mesh['date'=4,'path'=8] {'path'}, use_global_device_ids=true, to_apply=%region_3.4 | all-reduce | flops 512 | bytes 4096 | tf_op jit(solution)/shard_map/psum | solution.py:115
  230.5 0.6 broadcast_multiply_fusion
  (2 shorter events, 0.0 us)
Async XLA Ops:
  7.2 4.2 %copy-start = (bf16[128,16]{0,1:T(8,128)(2,1)S(1)}, bf16[128,16]{0,1:T(8,128)(2,1)}, u32[]{:S(2)}) copy-start(bf16[128,16]{0,1:T(8,128)(2,1)} %param.9) | copy-start | bytes 12292
  7.2 83.3 %all-reduce.3.cloned.1.call-start = ((), (), s32[]{:S(2)}) async-start(), calls=%async_computation | async-start | bytes 2097152 | tf_op jit(solution)/shard_map/psum | solution.py:99
  8.2 195.8 %collective-permute-start.1 = (bf16[2,16,4096]{2,1,0:T(8,128)(2,1)S(1)}, bf16[2,16,4096]{2,1,0:T(8,128)(2,1)S(1)}, u32[]{:S(2)}, u32[]{:S(2)}) collective-permute-start(bf16[2,16,4096]{2,1,0:T(8,128)(2,1)S(1)} %slice.13), channel_id=1, source_target_pairs={{0,8},{8,16},{16,24},{1,9},{9,17},{17,25},{2,10},{10,18},{18,26},{... | collective-permute-start | bytes 786440 | tf_op jit(solution)/shard_map/ppermute | solution.py:27
  23.0 3.6 %copy-start.1 = (bf16[8,128,4096]{1,2,0:T(8,128)(2,1)}, bf16[8,128,4096]{1,2,0:T(8,128)(2,1)S(1)}, u32[]{:S(2)}) copy-start(bf16[8,128,4096]{1,2,0:T(8,128)(2,1)S(1)} %add_convert_fusion) | copy-start | bytes 25165828
  26.5 5.7 %copy-start.2 = (s32[64]{0:T(128)S(1)}, s32[64]{0:T(128)}, u32[]{:S(2)}) copy-start(s32[64]{0:T(128)} %param.11) | copy-start | bytes 772
  26.5 5.7 %copy-start.3 = (s32[64]{0:T(128)S(1)}, s32[64]{0:T(128)}, u32[]{:S(2)}) copy-start(s32[64]{0:T(128)} %param.12) | copy-start | bytes 772
  26.5 5.7 %copy-start.4 = (s32[64]{0:T(128)S(1)}, s32[64]{0:T(128)}, u32[]{:S(2)}) copy-start(s32[64]{0:T(128)} %param.13) | copy-start | bytes 772
  32.2 171.8 %copy-start.5 = (f32[128]{0:T(128)S(1)}, f32[128]{0:T(128)}, u32[]{:S(2)}) copy-start(f32[128]{0:T(128)} %param.10) | copy-start | bytes 1540
  192.2 11.8 %collective-permute-start = (bf16[2,128,64]{2,1,0:T(8,128)(2,1)S(1)}, bf16[2,128,64]{2,1,0:T(8,128)(2,1)S(1)}, u32[]{:S(2)}, u32[]{:S(2)}) collective-permute-start(bf16[2,128,64]{2,1,0:T(8,128)(2,1)S(1)} %slice.16), channel_id=1, source_target_pairs={{0,8},{8,16},{16,24},{1,9},{9,17},{17,25},{2,10},{10,18},{18,26},{... | collective-permute-start | bytes 98312 | tf_op jit(solution)/shard_map/ppermute | solution.py:27
Sparse Core Ops, SparseCore 0:
  32.3 58.0 all-reduce.2
